TPU v7x, 256 devices: a whole 4x4x8 slice. The times are simulated.
256 devices in a mesh: dp: 32 (over z_lo, x, core), mp: 8 (over z_hi, y).
Axes of the slice: x: 4, y: 4, z: 8 (z_hi: 2, z_lo: 4; z = z_hi * 4 + z_lo), core: 2. Of those that a mesh axis runs over, the one named last changes fastest.
Arguments:
- queries: bfloat16 [24576, 1024], P('dp', 'mp'), may hold values from -3 to 3
- passages: bfloat16 [24576, 1024], P('dp', 'mp'), may hold values from -3 to 3
- positive: int32 [24576], P('dp'), may hold values from 0 to 24575
Outputs:
- grad_queries: bfloat16 [24576, 1024], P('dp', 'mp')
- grad_passages: bfloat16 [24576, 1024], P('dp', 'mp')
All inputs are finite; a program needn't handle non-finite values.
Results may differ from a plain program's by a relative error of at most 0.0034.
Values may be sent and summed in bfloat16 or wider, within the bound.
A program may use at most 128 MiB of HBM per device.

v0:
```python
import math
import jax
import jax.numpy as jnp
from jax import lax
from jax.sharding import Mesh
from jax.sharding import PartitionSpec as P

MP = ("mp_0", "mp_1")


def sent_to_all(array, axis):
    copies = jnp.broadcast_to(array, (lax.axis_size(axis), *array.shape))
    return lax.all_to_all(copies, axis, split_axis=0, concat_axis=0, tiled=True)


def collected_together(array, axis):
    leaves = jax.tree.leaves(array)
    turns = sorted(range(len(leaves)), key=lambda k: -leaves[k].size)
    width = (1, *leaves[turns[0]].shape)[-1]
    lines = [
        jnp.pad(leaves[k].reshape(-1), (0, -leaves[k].size % width)).reshape(-1, width)
        for k in turns
    ]
    both, at, found = (sent_to_all(jnp.concatenate(lines), axis), 0, {})
    for k, line in zip(turns, lines):
        slab = both[:, at : at + len(line)].reshape(len(both), -1)
        found[k] = slab[:, : leaves[k].size].reshape(-1, *leaves[k].shape)
        at += len(line)
    numbers = iter(range(len(leaves)))
    return jax.tree.map(lambda _: found[next(numbers)], array)


def joined_by_halves(pieces, combine):
    while len(jax.tree.leaves(pieces)[0]) > 1:
        pieces = jax.vmap(combine)(
            *(jax.tree.map(lambda part: part[side::2], pieces) for side in (0, 1))
        )
    return jax.tree.map(lambda part: part[0], pieces)


def joined_all(array, axis, combine):
    pieces = collected_together(array, axis)
    return joined_by_halves(pieces, combine)


def sum_in_order(pieces, axes, turns):
    shape = [lax.axis_size(a) for a in axes]
    pieces = pieces.reshape(*shape, *pieces.shape[1:])
    pieces = pieces.transpose(*turns, *range(len(axes), pieces.ndim))
    pieces = pieces.reshape(-1, *pieces.shape[len(axes) :])
    for k in turns:
        pieces = lax.psum_scatter(pieces, axes[k], scatter_dimension=0, tiled=True)
    return pieces[0]


def in_blocks(array, dim, count):
    before, after = (array.shape[:dim], array.shape[dim + 1 :])
    return jnp.moveaxis(array.reshape(*before, count, -1, *after), dim, 0)


def scatter_axes(array, axes, turns, dim):
    count = lax.axis_size(axes)
    return sum_in_order(in_blocks(array, dim, count), axes, turns)


def combine(first, second):
    highest = jnp.maximum(first[0], second[0])
    merged = first[1] * jnp.exp(first[0] - highest) + second[1] * jnp.exp(second[0] - highest)
    return (highest, merged)


def local(queries, passages, positive):
    group_rows, slice_width = queries.shape
    group_count = lax.axis_size("dp")
    model_index = lax.axis_index(MP)
    relaid = lax.all_to_all(passages, MP, split_axis=0, concat_axis=1, tiled=True)
    short_rows = relaid.shape[0]
    wide_queries = lax.all_gather(queries, MP, axis=1, tiled=True)
    passage_block = lax.all_gather(relaid, "dp", axis=0, tiled=True)
    full_width = wide_queries.shape[1]
    logit_scale = 3.0 / math.sqrt(full_width)
    scores = (
        lax.dot_general(
            wide_queries,
            passage_block,
            (((1,), (1,)), ((), ())),
            preferred_element_type=jnp.float32,
        )
        * logit_scale
    )
    local_max = jnp.max(scores, axis=1)
    local_total = jnp.sum(jnp.exp(scores - local_max[:, None]), axis=1)
    highest, row_total = joined_all((local_max, local_total), MP, combine)
    log_total = highest + jnp.log(row_total)
    column_pos = jnp.arange(group_count * short_rows, dtype=jnp.int32)
    column_ids = (
        column_pos // short_rows * group_rows + model_index * short_rows + column_pos % short_rows
    )
    onehot = (column_ids[None, :] == positive[:, None]).astype(jnp.float32)
    softmax_grad = (jnp.exp(scores - log_total[:, None]) - onehot).astype(jnp.bfloat16)
    query_terms = jnp.dot(softmax_grad, passage_block, preferred_element_type=jnp.float32)
    grad_queries = scatter_axes(query_terms, MP, (1, 0), 1).astype(jnp.bfloat16)
    summed = lax.psum_scatter(
        lax.dot_general(
            softmax_grad, wide_queries, (((0,), (0,)), ((), ())), preferred_element_type=jnp.float32
        ),
        "dp",
        scatter_dimension=0,
        tiled=True,
    )
    grad_passages = lax.all_to_all(
        summed.astype(jnp.bfloat16), MP, split_axis=1, concat_axis=0, tiled=True
    )
    return (grad_queries, grad_passages)


def solution(mesh):
    finer = Mesh(mesh.devices.reshape(mesh.shape["dp"], 2, 4), ("dp", "mp_0", "mp_1"))
    return jax.shard_map(
        local,
        mesh=finer,
        in_specs=(P("dp", MP), P("dp", MP), P("dp")),
        out_specs=(P("dp", MP), P("dp", MP)),
        check_vma=False,
    )
```

profile of v0, /device:TPU:1, one launch (start us, length us, event | category | flops | bytes accessed | tf_op | source)
XLA Modules:
  0.0 441.5 jit_solution(9130345755610493085)
XLA Ops:
  7.2 0.0 all-gather.3.cloned.1.call-start
  7.2 0.7 all-gather.3.cloned.1.call-update
  7.9 0.0 all-gather.5.cloned.1.call-start
  7.9 21.4 %all_to_all.43 = bf16[8,96,128]{2,1,0:T(8,128)(2,1)S(1)} all-to-all(bf16[8,96,128]{2,1,0:T(8,128)(2,1)} %bitcast.38), channel_id=1, replica_groups=mesh['dp'=32,'mp_0'=2,'mp_1'=4] {'mp_0','mp_1'}, dimensions={0} | all-to-all | bytes 393216 | tf_op jit(solution)/shard_map/all_to_all | solution.py:76
  29.4 0.7 copy_bitcast_fusion
  30.1 0.0 all-gather.5.cloned.1.call-update
  30.1 49.0 %all-gather.3.cloned.1.call-done = bf16[768,1024]{1,0:T(8,128)(2,1)} async-done(((bf16[768,128]{1,0:T(8,128)(2,1)}), bf16[768,1024]{1,0:T(8,128)(2,1)}) %all-gather.3.cloned.1.call-update) | async-done | bytes 1572880 | tf_op jit(solution)/shard_map/all_gather | solution.py:78
  79.1 68.8 %all-gather.5.cloned.1.call-done = bf16[3072,1024]{1,0:T(8,128)(2,1)} async-done(((bf16[96,1024]{1,0:T(8,128)(2,1)}), bf16[3072,1024]{1,0:T(8,128)(2,1)}) %all-gather.5.cloned.1.call-update) | async-done | bytes 6291472 | tf_op jit(solution)/shard_map/all_gather | solution.py:79
  147.9 7.8 %multiply_reduce_fusion = (f32[768]{0:T(1024)S(1)}, f32[768,3072]{1,0:T(8,128)S(1)}) fusion(bf16[768,1024]{1,0:T(8,128)(2,1)} %all-gather.3.cloned.1.call-done, bf16[3072,1024]{1,0:T(8,128)(2,1)} %all-gather.5.cloned.1.call-done), kind=kOutput, calls=%fused_computation.2 | convolution fusion | flops 4836555776 | bytes 17304576 | tf_op jit(solution)/shard_map/dot_general | solution.py:83
  155.8 0.0 copy-start.2
  155.8 3.5 copy-done
  159.3 1.7 exponential_reduce_fusion
  161.0 0.6 broadcast_in_dim.2
  161.6 7.9 %all-to-all-start.1 = ((f32[8,2,768]{2,1,0:T(2,128)}), f32[8,2,768]{2,1,0:T(2,128)S(1)}, u32[]{:S(2)}, u32[]{:S(2)}) async-start(f32[8,2,768]{2,1,0:T(2,128)} %broadcast_in_dim.2), calls=%async_computation.1 | async-start | bytes 98304 | tf_op jit(solution)/shard_map/all_to_all | solution.py:13
  169.5 0.0 reduce-scatter.4.cloned.1.call-start
  169.6 9.0 %all-to-all-done.1 = f32[8,2,768]{2,1,0:T(2,128)S(1)} async-done(((f32[8,2,768]{2,1,0:T(2,128)}), f32[8,2,768]{2,1,0:T(2,128)S(1)}, u32[]{:S(2)}, u32[]{:S(2)}) %all-to-all-start.1) | async-done | bytes 49184 | tf_op jit(solution)/shard_map/all_to_all | solution.py:13
  178.9 9.8 %convolution_bitcast_fusion = f32[96,8,8,128]{3,1,2,0:T(8,128)S(1)} fusion(bf16[3072,1024]{1,0:T(8,128)(2,1)} %all-gather.5.cloned.1.call-done, f32[768,3072]{1,0:T(8,128)} %copy-done, s32[3072]{0:T(1024)S(1)} %fusion.8, f32[768]{0:T(1024)S(1)} %add_reduce_fusion, s32[768]{0:T(1024)S(1)} %copy-done.2), kind=kOutput, calls=%fused_computation.3 | convolution fusion | flops 4845993984 | bytes 18892800 | tf_op jit(solution)/shard_map/dot_general | solution.py:101
  188.8 0.7 copy.20
  189.5 2.2 copy.14
  191.7 0.0 reduce-scatter.4.cloned.1.call-update
  191.8 0.0 reduce-scatter.8.cloned.1.call-start
  191.8 11.1 %fusion.12 = f32[3072,1024]{1,0:T(8,128)} fusion(bf16[768,1024]{1,0:T(8,128)(2,1)S(1)} %copy-done.1, f32[768,3072]{1,0:T(8,128)} %copy-done, s32[3072]{0:T(1024)S(1)} %fusion.8, f32[768]{0:T(1024)S(1)} %add_reduce_fusion, s32[768]{0:T(1024)S(1)} %copy-done.2), kind=kOutput, calls=%fused_computation.33 | convolution fusion | flops 4845993984 | bytes 23611392 | tf_op jit(solution)/shard_map/dot_general | solution.py:104
  202.9 0.0 reduce-scatter.8.cloned.1.call-update
  202.9 0.0 reduce-scatter.6.cloned.1.call-start
  203.0 25.3 %reduce-scatter.4.cloned.1.call-done = f32[2,768,128]{2,1,0:T(8,128)} async-done(((f32[8,768,128]{2,1,0:T(8,128)}), f32[2,768,128]{2,1,0:T(8,128)}) %reduce-scatter.4.cloned.1.call-update) | async-done | bytes 786448 | tf_op jit(solution)/shard_map/reduce_scatter | solution.py:52
  228.2 0.0 reduce-scatter.6.cloned.1.call-update
  228.3 164.2 %reduce-scatter.8.cloned.1.call-done = f32[96,1024]{1,0:T(8,128)} async-done(((f32[3072,1024]{1,0:T(8,128)}), f32[96,1024]{1,0:T(8,128)}) %reduce-scatter.8.cloned.1.call-update) | async-done | bytes 393232 | tf_op jit(solution)/shard_map/reduce_scatter | solution.py:103
  392.4 1.7 copy_bitcast_fusion.1
  394.1 8.7 %all-to-all-start.2 = ((bf16[96,8,128]{2,0,1:T(8,128)(2,1)}), bf16[96,8,128]{2,0,1:T(8,128)(2,1)S(1)}, u32[]{:S(2)}, u32[]{:S(2)}) async-start(bf16[96,8,128]{2,0,1:T(8,128)(2,1)} %copy_bitcast_fusion.1), calls=%async_computation.5 | async-start | bytes 393216 | tf_op jit(solution)/shard_map/all_to_all | solution.py:111
  402.8 29.8 %reduce-scatter.6.cloned.1.call-done = f32[1,768,128]{2,1,0:T(8,128)} async-done(((f32[2,768,128]{2,1,0:T(8,128)}), f32[1,768,128]{2,1,0:T(8,128)}) %reduce-scatter.6.cloned.1.call-update) | async-done | bytes 393232 | tf_op jit(solution)/shard_map/reduce_scatter | solution.py:52
  432.6 1.7 convert_bitcast_fusion.1
  434.3 0.7 copy.26
  (22 shorter events, 0.4 us)
Async XLA Ops:
  7.2 71.9 %all-gather.3.cloned.1.call-start = ((), (), s32[]{:S(2)}) async-start(), calls=%async_computation.6 | async-start | bytes 1769472 | tf_op jit(solution)/shard_map/all_gather | solution.py:78
  7.9 140.0 %all-gather.5.cloned.1.call-start = ((), (), s32[]{:S(2)}) async-start(), calls=%async_computation.7 | async-start | bytes 6488064 | tf_op jit(solution)/shard_map/all_gather | solution.py:79
  155.7 3.5 copy-start
  155.8 23.2 %copy-start.2 = (s32[768]{0:T(1024)S(1)}, s32[768]{0:T(1024)}, u32[]{:S(2)}) copy-start(s32[768]{0:T(1024)} %param.5) | copy-start | bytes 9220
  161.6 17.0 %all-to-all-start.1 = ((f32[8,2,768]{2,1,0:T(2,128)}), f32[8,2,768]{2,1,0:T(2,128)S(1)}, u32[]{:S(2)}, u32[]{:S(2)}) async-start(f32[8,2,768]{2,1,0:T(2,128)} %broadcast_in_dim.2), calls=%async_computation.1 | async-start | bytes 98304 | tf_op jit(solution)/shard_map/all_to_all | solution.py:13
  169.5 58.7 %reduce-scatter.4.cloned.1.call-start = ((), (), s32[]{:S(2)}) async-start(), calls=%async_computation.8 | async-start | bytes 3932160 | tf_op jit(solution)/shard_map/reduce_scatter | solution.py:52
  188.7 3.1 copy-start.1
  191.8 200.7 %reduce-scatter.8.cloned.1.call-start = ((), (), s32[]{:S(2)}) async-start(), calls=%async_computation.10 | async-start | bytes 12976128 | tf_op jit(solution)/shard_map/reduce_scatter | solution.py:103
  202.9 229.7 %reduce-scatter.6.cloned.1.call-start = ((), (), s32[]{:S(2)}) async-start(), calls=%async_computation.9 | async-start | bytes 1179648 | tf_op jit(solution)/shard_map/reduce_scatter | solution.py:52
  394.1 40.2 %all-to-all-start.2 = ((bf16[96,8,128]{2,0,1:T(8,128)(2,1)}), bf16[96,8,128]{2,0,1:T(8,128)(2,1)S(1)}, u32[]{:S(2)}, u32[]{:S(2)}) async-start(bf16[96,8,128]{2,0,1:T(8,128)(2,1)} %copy_bitcast_fusion.1), calls=%async_computation.5 | async-start | bytes 393216 | tf_op jit(solution)/shard_map/all_to_all | solution.py:111
Sparse Core Ops, SparseCore 0:
  10.4 68.6 all-gather.2
  81.5 66.3 all-gather.4
  191.9 36.3 reduce-scatter.3
  230.7 161.7 reduce-scatter.7
  394.8 37.7 reduce-scatter.5
where the time goes:
time: 442 us
  waiting for transfers between devices  347 us (79%)
  matrix products  28.7 us (6%)
  blocking collectives  21.4 us (5%)
  starting transfers between devices  16.8 us (4%)
  between operations  13.9 us (3%)
  local copies, waits for them, and re-layouts  8.76 us (2%)
  other arithmetic  5.15 us (1%)
    reduce_scatter x1, waiting for transfers between devices, local(): lax.psum_scatter(lax.dot_general(softmax_grad, wide_queries, (((0,), (0,)...  164 us
    all_gather x1, waiting for transfers between devices, local(): passage_block = lax.all_gather(relaid, 'dp', axis=0, tiled=True)  68.8 us
    reduce_scatter x2, waiting for transfers between devices, sum_in_order(): pieces = lax.psum_scatter(pieces, axes[k], scatter_dimension=0, tiled=True)  55.1 us
    all_gather x1, waiting for transfers between devices, local(): wide_queries = lax.all_gather(queries, MP, axis=1, tiled=True)  49 us
    all_to_all x1, blocking collectives, local(): lax.all_to_all(passages, MP, split_axis=0, concat_axis=1, tiled=True)  21.4 us
    dot_general x1, matrix products, local(): lax.dot_general(softmax_grad, wide_queries, (((0,), (0,)), ((), ())), pre...  11.1 us
    dot_general x1, matrix products, local(): jnp.dot(softmax_grad, passage_block, preferred_element_type=jnp.float32)  9.83 us
    all_to_all x1, waiting for transfers between devices, sent_to_all(): return lax.all_to_all(copies, axis, split_axis=0, concat_axis=0, tiled=True)  9 us
  transfers between devices with their start and end apart: 7, of which 6 were waited for; matrix products, arithmetic and copies ran while one was open for 3% of the time, Pallas kernels for 0%

commit v1 on v0

--- a/solution.py
+++ b/solution.py
@@ -75,7 +75,9 @@
     model_index = lax.axis_index(MP)
     relaid = lax.all_to_all(passages, MP, split_axis=0, concat_axis=1, tiled=True)
     short_rows = relaid.shape[0]
-    wide_queries = lax.all_gather(queries, MP, axis=1, tiled=True)
+    wide_queries = jnp.concatenate(
+        lax.all_to_all(jnp.stack([queries] * lax.axis_size(MP)), MP, 0, 0), axis=1
+    )
     passage_block = lax.all_gather(relaid, "dp", axis=0, tiled=True)
     full_width = wide_queries.shape[1]
     logit_scale = 3.0 / math.sqrt(full_width)

time: 442 us -> 416 us (0.941)
  waiting for transfers between devices: 347 us -> 315 us
    all_gather x1 -> x0, waiting for transfers between devices: 49 us -> none  [local(): wide_queries = lax.all_gather(queries, MP, axis=1, tiled=True)]
    all_to_all x0 -> x1, waiting for transfers between devices: none -> 42.4 us  [local(): lax.all_to_all(jnp.stack([queries] * lax.axis_size(MP)), MP, 0, 0)]
    all_gather x1, waiting for transfers between devices: 68.8 us -> 43.3 us  [local(): passage_block = lax.all_gather(relaid, 'dp', axis=0, tiled=True)]
  transfers between devices with their start and end apart: 7 -> 7, of which waited for: 6 -> 6; matrix products, arithmetic and copies ran while one was open for 3% -> 4% of each run, Pallas kernels for 0% -> 0%
where the time goes in v1:
time: 416 us; the launch traced here: 415 us
  waiting for transfers between devices  315 us (76%)
  matrix products  28.2 us (7%)
  blocking collectives  21.4 us (5%)
  starting transfers between devices  20.5 us (5%)
  between operations  13.9 us (3%)
  local copies, waits for them, and re-layouts  11.1 us (3%)
  other arithmetic  5.15 us (1%)
    reduce_scatter x1, waiting for transfers between devices, local(): lax.psum_scatter(lax.dot_general(softmax_grad, wide_queries, (((0,), (0,)...  165 us
    reduce_scatter x2, waiting for transfers between devices, sum_in_order(): pieces = lax.psum_scatter(pieces, axes[k], scatter_dimension=0, tiled=True)  55.6 us
    all_gather x1, waiting for transfers between devices, local(): passage_block = lax.all_gather(relaid, 'dp', axis=0, tiled=True)  43.3 us
    all_to_all x1, waiting for transfers between devices, local(): lax.all_to_all(jnp.stack([queries] * lax.axis_size(MP)), MP, 0, 0)  42.4 us
    all_to_all x1, blocking collectives, local(): lax.all_to_all(passages, MP, split_axis=0, concat_axis=1, tiled=True)  21.4 us
    dot_general x1, matrix products, local(): lax.dot_general(softmax_grad, wide_queries, (((0,), (0,)), ((), ())), pre...  11 us
    dot_general x1, matrix products, local(): jnp.dot(softmax_grad, passage_block, preferred_element_type=jnp.float32)  9.83 us
    all_to_all x1, waiting for transfers between devices, sent_to_all(): return lax.all_to_all(copies, axis, split_axis=0, concat_axis=0, tiled=True)  9 us
  transfers between devices with their start and end apart: 7, of which 6 were waited for; matrix products, arithmetic and copies ran while one was open for 4% of the time, Pallas kernels for 0%

profile of v1, /device:TPU:1, one launch (start us, length us, event | category | flops | bytes accessed | tf_op | source)
XLA Modules:
  0.0 415.4 jit_solution(9041479515898635664)
XLA Ops:
  7.2 0.0 all-gather.2.cloned.1.call-start
  7.2 21.4 %all_to_all.48 = bf16[8,96,128]{2,1,0:T(8,128)(2,1)S(1)} all-to-all(bf16[8,96,128]{2,1,0:T(8,128)(2,1)} %bitcast.43), channel_id=1, replica_groups=mesh['dp'=32,'mp_0'=2,'mp_1'=4] {'mp_0','mp_1'}, dimensions={0} | all-to-all | bytes 393216 | tf_op jit(solution)/shard_map/all_to_all | solution.py:76
  28.6 0.7 copy_bitcast_fusion
  29.3 0.0 all-gather.2.cloned.1.call-update
  29.4 1.1 copy.13
  30.4 1.2 stack.2
  31.7 3.6 all-to-all-start
  35.3 42.4 %all-to-all-done = bf16[8,768,128]{1,2,0:T(8,128)(2,1)S(1)} async-done(((bf16[8,768,128]{1,2,0:T(8,128)(2,1)}), bf16[8,768,128]{1,2,0:T(8,128)(2,1)S(1)}, u32[]{:S(2)}, u32[]{:S(2)}) %all-to-all-start) | async-done | bytes 1572896 | tf_op jit(solution)/shard_map/all_to_all | solution.py:79
  77.7 43.3 %all-gather.2.cloned.1.call-done = bf16[3072,1024]{1,0:T(8,128)(2,1)} async-done(((bf16[96,1024]{1,0:T(8,128)(2,1)}), bf16[3072,1024]{1,0:T(8,128)(2,1)}) %all-gather.2.cloned.1.call-update) | async-done | bytes 6291472 | tf_op jit(solution)/shard_map/all_gather | solution.py:81
  121.0 7.4 %multiply_reduce_fusion = (f32[768]{0:T(1024)S(1)}, f32[768,3072]{1,0:T(8,128)S(1)}) fusion(bf16[768,1024]{0,1:T(8,128)(2,1)S(1)} %bitcast.40, bf16[3072,1024]{1,0:T(8,128)(2,1)} %all-gather.2.cloned.1.call-done), kind=kOutput, calls=%fused_computation.2 | convolution fusion | flops 4836555776 | bytes 17304576 | tf_op jit(solution)/shard_map/dot_general | solution.py:85
  128.4 3.5 copy-done
  131.9 1.7 exponential_reduce_fusion
  133.6 0.6 broadcast_in_dim.2
  134.2 8.7 %all-to-all-start.2 = ((f32[8,2,768]{2,1,0:T(2,128)}), f32[8,2,768]{2,1,0:T(2,128)S(1)}, u32[]{:S(2)}, u32[]{:S(2)}) async-start(f32[8,2,768]{2,1,0:T(2,128)} %broadcast_in_dim.2), calls=%async_computation.2 | async-start | bytes 98304 | tf_op jit(solution)/shard_map/all_to_all | solution.py:13
  142.9 0.0 reduce-scatter.4.cloned.1.call-start
  143.0 9.0 %all-to-all-done.2 = f32[8,2,768]{2,1,0:T(2,128)S(1)} async-done(((f32[8,2,768]{2,1,0:T(2,128)}), f32[8,2,768]{2,1,0:T(2,128)S(1)}, u32[]{:S(2)}, u32[]{:S(2)}) %all-to-all-start.2) | async-done | bytes 49184 | tf_op jit(solution)/shard_map/all_to_all | solution.py:13
  152.3 9.8 %convolution_bitcast_fusion = f32[96,8,8,128]{3,1,2,0:T(8,128)S(1)} fusion(bf16[3072,1024]{1,0:T(8,128)(2,1)} %all-gather.2.cloned.1.call-done, f32[768,3072]{1,0:T(8,128)} %copy-done, s32[3072]{0:T(1024)S(1)} %fusion.8, f32[768]{0:T(1024)S(1)} %add_reduce_fusion, s32[768]{0:T(1024)S(1)} %copy-done.1), kind=kOutput, calls=%fused_computation.3 | convolution fusion | flops 4845993984 | bytes 18892800 | tf_op jit(solution)/shard_map/dot_general | solution.py:103
  162.2 0.7 copy.22
  162.9 2.2 copy.16
  165.2 0.0 reduce-scatter.4.cloned.1.call-update
  165.2 0.2 reduce-scatter.8.cloned.1.call-start
  165.4 11.0 %fusion.12 = f32[3072,1024]{1,0:T(8,128)} fusion(bf16[768,1024]{0,1:T(8,128)(2,1)S(1)} %bitcast.41, f32[768,3072]{1,0:T(8,128)} %copy-done, s32[3072]{0:T(1024)S(1)} %fusion.8, f32[768]{0:T(1024)S(1)} %add_reduce_fusion, s32[768]{0:T(1024)S(1)} %copy-done.1), kind=kOutput, calls=%fused_computation.33 | convolution fusion | flops 4845993984 | bytes 23611392 | tf_op jit(solution)/shard_map/dot_general | solution.py:106
  176.5 0.0 reduce-scatter.8.cloned.1.call-update
  176.5 0.0 reduce-scatter.6.cloned.1.call-start
  176.5 25.8 %reduce-scatter.4.cloned.1.call-done = f32[2,768,128]{2,1,0:T(8,128)} async-done(((f32[8,768,128]{2,1,0:T(8,128)}), f32[2,768,128]{2,1,0:T(8,128)}) %reduce-scatter.4.cloned.1.call-update) | async-done | bytes 786448 | tf_op jit(solution)/shard_map/reduce_scatter | solution.py:52
  202.3 0.0 reduce-scatter.6.cloned.1.call-update
  202.4 164.7 %reduce-scatter.8.cloned.1.call-done = f32[96,1024]{1,0:T(8,128)} async-done(((f32[3072,1024]{1,0:T(8,128)}), f32[96,1024]{1,0:T(8,128)}) %reduce-scatter.8.cloned.1.call-update) | async-done | bytes 393232 | tf_op jit(solution)/shard_map/reduce_scatter | solution.py:105
  367.1 1.7 copy_bitcast_fusion.1
  368.8 7.9 %all-to-all-start.3 = ((bf16[96,8,128]{2,0,1:T(8,128)(2,1)}), bf16[96,8,128]{2,0,1:T(8,128)(2,1)S(1)}, u32[]{:S(2)}, u32[]{:S(2)}) async-start(bf16[96,8,128]{2,0,1:T(8,128)(2,1)} %copy_bitcast_fusion.1), calls=%async_computation.6 | async-start | bytes 393216 | tf_op jit(solution)/shard_map/all_to_all | solution.py:113
  376.7 29.8 %reduce-scatter.6.cloned.1.call-done = f32[1,768,128]{2,1,0:T(8,128)} async-done(((f32[2,768,128]{2,1,0:T(8,128)}), f32[1,768,128]{2,1,0:T(8,128)}) %reduce-scatter.6.cloned.1.call-update) | async-done | bytes 393232 | tf_op jit(solution)/shard_map/reduce_scatter | solution.py:52
  406.5 1.7 convert_bitcast_fusion.1
  408.2 0.7 copy.28
  (21 shorter events, 0.4 us)
Async XLA Ops:
  7.2 113.8 %all-gather.2.cloned.1.call-start = ((), (), s32[]{:S(2)}) async-start(), calls=%async_computation.7 | async-start | bytes 6488064 | tf_op jit(solution)/shard_map/all_gather | solution.py:81
  31.7 46.0 %all-to-all-start = ((bf16[8,768,128]{1,2,0:T(8,128)(2,1)}), bf16[8,768,128]{1,2,0:T(8,128)(2,1)S(1)}, u32[]{:S(2)}, u32[]{:S(2)}) async-start(bf16[8,768,128]{1,2,0:T(8,128)(2,1)} %stack.2), calls=%async_computation | async-start | bytes 3145728 | tf_op jit(solution)/shard_map/all_to_all | solution.py:79
  128.3 3.6 copy-start
  128.3 24.0 %copy-start.1 = (s32[768]{0:T(1024)S(1)}, s32[768]{0:T(1024)}, u32[]{:S(2)}) copy-start(s32[768]{0:T(1024)} %param.5) | copy-start | bytes 9220
  134.2 17.8 %all-to-all-start.2 = ((f32[8,2,768]{2,1,0:T(2,128)}), f32[8,2,768]{2,1,0:T(2,128)S(1)}, u32[]{:S(2)}, u32[]{:S(2)}) async-start(f32[8,2,768]{2,1,0:T(2,128)} %broadcast_in_dim.2), calls=%async_computation.2 | async-start | bytes 98304 | tf_op jit(solution)/shard_map/all_to_all | solution.py:13
  142.9 59.4 %reduce-scatter.4.cloned.1.call-start = ((), (), s32[]{:S(2)}) async-start(), calls=%async_computation.8 | async-start | bytes 3932160 | tf_op jit(solution)/shard_map/reduce_scatter | solution.py:52
  165.2 201.9 %reduce-scatter.8.cloned.1.call-start = ((), (), s32[]{:S(2)}) async-start(), calls=%async_computation.10 | async-start | bytes 12976128 | tf_op jit(solution)/shard_map/reduce_scatter | solution.py:105
  176.5 230.0 %reduce-scatter.6.cloned.1.call-start = ((), (), s32[]{:S(2)}) async-start(), calls=%async_computation.9 | async-start | bytes 1179648 | tf_op jit(solution)/shard_map/reduce_scatter | solution.py:52
  368.8 39.4 %all-to-all-start.3 = ((bf16[96,8,128]{2,0,1:T(8,128)(2,1)}), bf16[96,8,128]{2,0,1:T(8,128)(2,1)S(1)}, u32[]{:S(2)}, u32[]{:S(2)}) async-start(bf16[96,8,128]{2,0,1:T(8,128)(2,1)} %copy_bitcast_fusion.1), calls=%async_computation.6 | async-start | bytes 393216 | tf_op jit(solution)/shard_map/all_to_all | solution.py:113
Sparse Core Ops, SparseCore 0:
  29.5 91.4 all-gather.1
  165.3 36.9 reduce-scatter.3
  204.9 162.1 reduce-scatter.7
  369.4 37.0 reduce-scatter.5
